TPU v7x, 32 devices: a whole 2x2x4 slice. The times are simulated.
32 devices in a mesh: gx: 4 (over x, core), gy: 2 (over y), gz: 4 (over z).
Axes of the slice: x: 2, y: 2, z: 4, core: 2. Of those that a mesh axis runs over, the one named last changes fastest.
Arguments:
- start_field: float32 [256, 128, 1024], P('gx', 'gy', 'gz'), may hold values from -6 to 6
- right_side: float32 [256, 128, 1024], P('gx', 'gy', 'gz'), may hold values from -6 to 6
Outputs:
- corrected: float32 [256, 128, 1024], P('gx', 'gy', 'gz')
All inputs are finite; a program needn't handle non-finite values.
Results may differ from a plain program's by a relative error of at most 0.00002.
Values sent between devices are 32-bit elements; how exact they have to be, the bound alone decides.
A program may use at most 128 MiB of HBM per device.

v0:
```python
import functools

import jax
import jax.numpy as jnp
from jax import lax
from jax.experimental import pallas as pl
from jax.experimental.pallas import tpu as pltpu
from jax.sharding import PartitionSpec as P

FINE_SWEEPS = 2
COARSE_SWEEPS = 4
OMEGA = 6.0 / 7.0
STEP = OMEGA / 1.5
LANES = 128
PAD = 8
AXES = ("gx", "gy", "gz")
MESH = pl.DeviceIdType.MESH
HIGH = lax.Precision.HIGHEST

FACES = ((1, 0, 0), (-1, 0, 0), (0, 1, 0), (0, -1, 0), (0, 0, 1), (0, 0, -1))
EDGES = ((0, 1, 1), (1, 1, 0), (1, 0, 1), (1, 1, 1))
NEIGHBOURS = FACES + EDGES + tuple(tuple(-c for c in d) for d in EDGES)
N_COPIES = 6 * (FINE_SWEEPS + 1) + 4 + 6 * (COARSE_SWEEPS - 1) + 7


def rotated(values, shift):
    return pltpu.roll(values, shift, 1)


def correct_kernel(
    sizes, start_hbm, right_hbm, smooth_hbm, q_ref,
    u0, u1, u2, f, ys, yr, zs, zr, rs, rr, px, rys, ryr, rdr, rzs, rzr, rhs,
    c0, c1, c2, c3, cys, cyr, czs, czr, xyr, xzr, yzr, xyzr, ze,
    local_sem, send_sem, recv_sem,
):
    nt, nx, ny, _ = f.shape
    mx, my = nx // 2, ny // 2
    me = tuple(lax.axis_index(a) for a in AXES)
    lane = lax.broadcasted_iota(jnp.int32, (ny, LANES), 1)
    lane_c = lax.broadcasted_iota(jnp.int32, (my, LANES), 1)

    def there(d):
        found = None
        for at, step, size in zip(me, d, sizes):
            if step:
                one = at < size - 1 if step > 0 else at > 0
                found = one if found is None else jnp.logical_and(found, one)
        return found

    def minus(d):
        return tuple(-c for c in d)

    def device(d):
        return tuple(at + step for at, step in zip(me, d))

    sent = []

    def send(src, dst, d):
        number = len(sent)

        def copy(to):
            return pltpu.make_async_remote_copy(
                src_ref=src, dst_ref=dst, send_sem=send_sem.at[number],
                recv_sem=recv_sem.at[number], device_id=device(to), device_id_type=MESH)

        @pl.when(there(d))
        def _():
            copy(d).start()

        sent.append((copy, d, dst))
        return number

    def arrive(number):
        copy, d, dst = sent[number]

        @pl.when(there(minus(d)))
        def _():
            copy(minus(d)).wait_recv()

        @pl.when(jnp.logical_not(there(minus(d))))
        def _():
            dst[...] = jnp.zeros(dst.shape, dst.dtype)

    loads = []
    for t in range(nt):
        part = pl.ds(t * LANES, LANES)
        loads.append(pltpu.make_async_copy(
            start_hbm.at[:, :, part], u0.at[t, pl.ds(1, nx), pl.ds(PAD, ny), :], local_sem.at[t]))
    for t in range(nt):
        part = pl.ds(t * LANES, LANES)
        loads.append(pltpu.make_async_copy(right_hbm.at[:, :, part], f.at[t], local_sem.at[nt + t]))
    for load in loads:
        load.start()

    barrier = pltpu.get_barrier_semaphore()
    expected = jnp.int32(0)
    for d in NEIGHBOURS:
        @pl.when(there(d))
        def _():
            pl.semaphore_signal(barrier, inc=1, device_id=device(d), device_id_type=MESH)
        expected = expected + there(d).astype(jnp.int32)
    pl.semaphore_wait(barrier, expected)

    mid = pl.ds(PAD, ny)

    def pack_fine(k, x, planes, packs):
        for t in range(nt):
            ys[k, 0, t, pl.ds(x, 1), :] = planes[t][0:1, :]
            ys[k, 1, t, pl.ds(x, 1), :] = planes[t][ny - 1:ny, :]
        low, high = packs
        low = jnp.where(lane == x, rotated(planes[0], x), low)
        high = jnp.where(lane == x, rotated(planes[nt - 1], x + 1), high)
        return low, high

    def send_x(u):
        return [
            send(u.at[:, nx, mid, :], u.at[:, 0, mid, :], (1, 0, 0)),
            send(u.at[:, 1, mid, :], u.at[:, nx + 1, mid, :], (-1, 0, 0)),
        ]

    def send_yz(k, packs):
        zs[k, 0], zs[k, 1] = packs
        return [
            send(ys.at[k, 1], yr.at[k, 0], (0, 1, 0)),
            send(ys.at[k, 0], yr.at[k, 1], (0, -1, 0)),
            send(zs.at[k, 1], zr.at[k, 0], (0, 0, 1)),
            send(zs.at[k, 0], zr.at[k, 1], (0, 0, -1)),
        ]

    def fill_fine(u, k):
        def rows(x, _):
            for t in range(nt):
                u[t, x + 1, PAD - 1:PAD, :] = yr[k, 0, t, pl.ds(x, 1), :]
                u[t, x + 1, PAD + ny:PAD + ny + 1, :] = yr[k, 1, t, pl.ds(x, 1), :]
            return 0
        lax.fori_loop(0, nx, rows, 0, unroll=4)

    def around(u, k, x):
        centers, sums = [], []
        low = rotated(zr[k, 0], lax.rem(LANES - x, LANES))
        high = rotated(zr[k, 1], LANES - 1 - x)
        planes = [u[t, x + 1, mid, :] for t in range(nt)]
        left = [rotated(p, 1) for p in planes]
        right = [rotated(p, LANES - 1) for p in planes]
        for t in range(nt):
            before = jnp.where(lane == 0, left[t - 1] if t else low, left[t])
            after = jnp.where(lane == LANES - 1, right[t + 1] if t < nt - 1 else high, right[t])
            total = u[t, x, mid, :] + u[t, x + 2, mid, :]
            total = total + u[t, x + 1, PAD - 1:PAD - 1 + ny, :] + u[t, x + 1, PAD + 1:PAD + 1 + ny, :]
            sums.append(total + before + after)
        return planes, sums

    zero_pack = (jnp.zeros((ny, LANES), jnp.float32),) * 2

    for load in loads[:nt]:
        load.wait()
    waits = send_x(u0)
    packs = lax.fori_loop(
        0, nx, lambda x, c: pack_fine(0, x, [u0[t, x + 1, mid, :] for t in range(nt)], c), zero_pack)
    waits += send_yz(0, packs)
    for load in loads[nt:]:
        load.wait()

    fields = (u0, u1, u2)
    for k in range(FINE_SWEEPS):
        old, new = fields[k], fields[k + 1]
        for number in waits:
            arrive(number)
        fill_fine(old, k)

        def sweep(x, packs):
            planes, sums = around(old, k, x)
            results = []
            for t in range(nt):
                value = (planes[t] + f[t, x] + sums[t]) * (1.0 - OMEGA)
                new[t, x + 1, mid, :] = value
                results.append(value)
            return pack_fine(k + 1, x, results, packs)

        packs = lax.fori_loop(0, nx, sweep, zero_pack)
        waits = send_x(new) + send_yz(k + 1, packs)

    smooth = fields[FINE_SWEEPS]
    outs = [
        pltpu.make_async_copy(
            smooth.at[t, pl.ds(1, nx), mid, :], smooth_hbm.at[:, :, pl.ds(t * LANES, LANES)],
            local_sem.at[2 * nt + t])
        for t in range(nt)
    ]
    for out in outs:
        out.start()
    for number in waits:
        arrive(number)
    fill_fine(smooth, FINE_SWEEPS)

    def residual(x):
        planes, sums = around(smooth, FINE_SWEEPS, x)
        return tuple(f[t, x] - 6.0 * planes[t] + sums[t] for t in range(nt))

    first = residual(0)
    for t in range(nt):
        rs[t] = first[t]
    rx = send(rs, rr, (-1, 0, 0))

    def restrict_x(at, even, odd, following):
        for t in range(nt):
            value = 0.25 * even[t] + 0.5 * odd[t] + 0.25 * following[t]
            px[t, at, 0:ny, :] = value
            rys[t, pl.ds(at, 1), :] = value[0:1, :]

    def step_x(i, even):
        odd = residual(2 * i + 1)
        following = residual(2 * i + 2)
        restrict_x(i, even, odd, following)
        return following

    even = lax.fori_loop(0, mx - 1, step_x, first)
    odd = residual(nx - 1)
    arrive(rx)
    restrict_x(mx - 1, even, odd, [rr[t] for t in range(nt)])
    ry = send(rys, ryr, (0, -1, 0))
    rd = send(rys, rdr, (0, -1, -1))

    row = lax.broadcasted_iota(jnp.int32, (LANES, LANES), 0)
    col = lax.broadcasted_iota(jnp.int32, (LANES, LANES), 1)

    def weights(fine, coarse, scale):
        gap = fine - 2 * coarse
        outer = jnp.logical_or(gap == 0, gap == 2)
        return jnp.where(gap == 1, 0.5 * scale, jnp.where(outer, 0.25 * scale, 0.0)).astype(jnp.float32)

    down = [weights(row + t * LANES, col, 1.0) for t in range(nt)]
    up = [weights(col + t * LANES, row, 2.0) for t in range(nt)]
    last_row = lax.broadcasted_iota(jnp.int32, (my, LANES), 0) == my - 1

    def step_y(i, pack):
        parts = []
        for t in range(nt):
            evens = px[t, i, pl.ds(0, my, stride=2), :]
            odds = px[t, i, pl.ds(1, my, stride=2), :]
            nexts = jnp.where(last_row, 0.0, pltpu.roll(evens, my - 1, 0))
            parts.append(0.25 * evens + 0.5 * odds + 0.25 * nexts)
        value = jnp.zeros((my, LANES), jnp.float32)
        for t in range(nt):
            value = value + jnp.dot(parts[t], down[t], precision=HIGH, preferred_element_type=jnp.float32)
        rhs[i] = value
        return jnp.where(lane_c == i, rotated(parts[0], i), pack)

    zero_c = jnp.zeros((my, LANES), jnp.float32)
    rzs[...] = lax.fori_loop(0, mx, step_y, zero_c, unroll=2)
    rz = send(rzs, rzr, (0, 0, -1))

    mid_c = pl.ds(PAD, my)

    def pack_coarse(k, i, plane, packs):
        cys[k, 0, pl.ds(i, 1), :] = plane[0:1, :]
        cys[k, 1, pl.ds(i, 1), :] = plane[my - 1:my, :]
        low, high = packs
        low = jnp.where(lane_c == i, rotated(plane, i), low)
        high = jnp.where(lane_c == i, rotated(plane, i + 1), high)
        return low, high

    def send_coarse(c, k, packs):
        czs[k, 0], czs[k, 1] = packs
        return [
            send(c.at[mx, mid_c, :], c.at[0, mid_c, :], (1, 0, 0)),
            send(c.at[1, mid_c, :], c.at[mx + 1, mid_c, :], (-1, 0, 0)),
            send(cys.at[k, 1], cyr.at[k, 0], (0, 1, 0)),
            send(cys.at[k, 0], cyr.at[k, 1], (0, -1, 0)),
            send(czs.at[k, 1], czr.at[k, 0], (0, 0, 1)),
            send(czs.at[k, 0], czr.at[k, 1], (0, 0, -1)),
        ]

    for number in (ry, rd, rz):
        arrive(number)
    lane_x = lax.broadcasted_iota(jnp.int32, (mx, LANES), 1)
    beyond = jnp.where(lane_x == LANES - 1, 0.0625 * rotated(rdr[0], LANES - 1), 0.0)
    for t in range(nt):
        beyond = beyond + 0.25 * jnp.dot(
            ryr[t], down[t], precision=HIGH, preferred_element_type=jnp.float32)
    cys[0, 0] = beyond

    def finish_rhs(i, packs):
        outside = 0.25 * rotated(rzr[...], LANES - 1 - i)
        value = rhs[i] + jnp.where(lane_c == LANES - 1, outside, 0.0)
        value = value + jnp.where(last_row, cys[0, 0, pl.ds(i, 1), :], 0.0)
        value = value * STEP
        rhs[i] = value
        c0[i + 1, mid_c, :] = value
        return pack_coarse(0, i, value, packs)

    packs = lax.fori_loop(0, mx, finish_rhs, (zero_c, zero_c), unroll=2)
    grids = (c0, c1, c2, c3)
    waits = send_coarse(c0, 0, packs)
    for k in range(COARSE_SWEEPS - 1):
        old, new = grids[k], grids[k + 1]
        for number in waits:
            arrive(number)

        def rows(i, _):
            old[i + 1, PAD - 1:PAD, :] = cyr[k, 0, pl.ds(i, 1), :]
            old[i + 1, PAD + my:PAD + my + 1, :] = cyr[k, 1, pl.ds(i, 1), :]
            return 0

        lax.fori_loop(0, mx, rows, 0, unroll=4)

        def sweep_c(i, packs):
            low = rotated(czr[k, 0], lax.rem(LANES - i, LANES))
            high = rotated(czr[k, 1], LANES - 1 - i)
            plane = old[i + 1, mid_c, :]
            total = old[i, mid_c, :] + old[i + 2, mid_c, :]
            total = total + old[i + 1, PAD - 1:PAD - 1 + my, :] + old[i + 1, PAD + 1:PAD + 1 + my, :]
            total = total + jnp.where(lane_c == 0, low, rotated(plane, 1))
            total = total + jnp.where(lane_c == LANES - 1, high, rotated(plane, LANES - 1))
            value = (1.0 - 1.5 * STEP) * plane + rhs[i] + (0.25 * STEP) * total
            new[i + 1, mid_c, :] = value
            return pack_coarse(k + 1, i, value, packs)

        packs = lax.fori_loop(0, mx, sweep_c, (zero_c, zero_c), unroll=2)
        if k < COARSE_SWEEPS - 2:
            waits = send_coarse(new, k + 1, packs)

    k = COARSE_SWEEPS - 1
    last = grids[k]
    czs[k, 1] = packs[1]
    waits = [
        send(last.at[mx, mid_c, :], last.at[0, mid_c, :], (1, 0, 0)),
        send(cys.at[k, 1], cyr.at[k, 0], (0, 1, 0)),
        send(czs.at[k, 1], czr.at[k, 0], (0, 0, 1)),
        send(cys.at[k, 1], xyr, (1, 1, 0)),
        send(czs.at[k, 1], xzr, (1, 0, 1)),
        send(czs.at[k, 1], yzr, (0, 1, 1)),
        send(czs.at[k, 1], xyzr, (1, 1, 1)),
    ]
    for number in waits:
        arrive(number)
    inside = jnp.where(lane_c == 0, rotated(xzr[...], LANES - mx + 1), rotated(czr[k, 0], 1))
    corner = jnp.where(lane_c == 0, rotated(xyzr[...], LANES - mx + 1), rotated(yzr[...], 1))
    ze[mid_c, :] = inside
    ze[0:PAD, :] = corner[my - PAD:my, :]
    last[0, 0:PAD, :] = jnp.broadcast_to(xyr[mx - 1:mx, :], (PAD, LANES))

    def rows_last(i, _):
        last[i + 1, 0:PAD, :] = jnp.broadcast_to(cyr[k, 0, pl.ds(i, 1), :], (PAD, LANES))
        return 0

    lax.fori_loop(0, mx, rows_last, 0, unroll=4)
    lane_e = lax.broadcasted_iota(jnp.int32, (my + PAD, LANES), 1)

    def prolong_z(p, _):
        plane = last[p, 0:PAD + my, :]
        outside = 0.5 * rotated(ze[...], lax.rem(LANES - p, LANES))
        for t in range(nt):
            value = jnp.dot(plane, up[t], precision=HIGH, preferred_element_type=jnp.float32)
            if t == 0:
                value = value + jnp.where(lane_e == 0, outside, 0.0)
            q_ref[p, t] = value
        return 0

    lax.fori_loop(0, mx + 1, prolong_z, 0)

    for copy, d, _ in sent:
        @pl.when(there(d))
        def _():
            copy(d).wait_send()
    for out in outs:
        out.wait()


def add_kernel(per, smooth_ref, q_ref, out_ref, both):
    nt, my = q_ref.shape[1], q_ref.shape[2] - PAD
    base = pl.program_id(0) * per

    def spread(j):
        for t in range(nt):
            here = q_ref[base + j, t, PAD:PAD + my, :]
            before = q_ref[base + j, t, PAD - 1:PAD - 1 + my, :]
            both[j, t, pl.ds(0, my, stride=2), :] = 0.5 * (before + here)
            both[j, t, pl.ds(1, my, stride=2), :] = here

    def run(j, _):
        spread(j)
        return 0

    def add(j, _):
        for t in range(nt):
            part = pl.ds(t * LANES, LANES)
            here = both[j + 1, t]
            out_ref[2 * j, :, part] = smooth_ref[2 * j, :, part] + 0.5 * (both[j, t] + here)
            out_ref[2 * j + 1, :, part] = smooth_ref[2 * j + 1, :, part] + here
        return 0

    lax.fori_loop(0, per + 1, run, 0)
    lax.fori_loop(0, per, add, 0)


def on_device(sizes, start_field, right_side):
    nx, ny, nz = start_field.shape
    nt, mx, my = nz // LANES, nx // 2, ny // 2
    f32 = jnp.float32
    fine = pltpu.VMEM((nt, nx + 2, ny + 2 * PAD, LANES), f32)
    coarse = pltpu.VMEM((mx + 2, my + 2 * PAD, LANES), f32)
    rounds = FINE_SWEEPS + 1
    y_faces = pltpu.VMEM((rounds, 2, nt, nx, LANES), f32)
    z_faces = pltpu.VMEM((rounds, 2, ny, LANES), f32)
    x_plane = pltpu.VMEM((nt, ny, LANES), f32)
    y_rows = pltpu.VMEM((nt, mx, LANES), f32)
    z_pack = pltpu.VMEM((my, LANES), f32)
    smooth, q = pl.pallas_call(
        functools.partial(correct_kernel, sizes),
        out_shape=(
            jax.ShapeDtypeStruct((nx, ny, nz), f32),
            jax.ShapeDtypeStruct((mx + 1, nt, my + PAD, LANES), f32),
        ),
        in_specs=[pl.BlockSpec(memory_space=pl.ANY)] * 2,
        out_specs=(pl.BlockSpec(memory_space=pl.ANY), pl.BlockSpec(memory_space=pltpu.VMEM)),
        scratch_shapes=[
            fine, fine, fine, pltpu.VMEM((nt, nx, ny, LANES), f32),
            y_faces, y_faces, z_faces, z_faces,
            x_plane, x_plane, pltpu.VMEM((nt, mx, ny, LANES), f32),
            y_rows, y_rows, y_rows, z_pack, z_pack, pltpu.VMEM((mx, my, LANES), f32),
            coarse, coarse, coarse, coarse,
            pltpu.VMEM((COARSE_SWEEPS, 2, mx, LANES), f32), pltpu.VMEM((COARSE_SWEEPS, 2, mx, LANES), f32),
            pltpu.VMEM((COARSE_SWEEPS, 2, my, LANES), f32), pltpu.VMEM((COARSE_SWEEPS, 2, my, LANES), f32),
            pltpu.VMEM((mx, LANES), f32), z_pack, z_pack, z_pack, pltpu.VMEM((my + PAD, LANES), f32),
            pltpu.SemaphoreType.DMA((3 * nt,)),
            pltpu.SemaphoreType.DMA((N_COPIES,)),
            pltpu.SemaphoreType.DMA((N_COPIES,)),
        ],
        compiler_params=pltpu.CompilerParams(
            collective_id=0, has_side_effects=True, vmem_limit_bytes=48 * 1024 * 1024),
    )(start_field, right_side)
    per = 8 if mx % 8 == 0 else 1
    block = pl.BlockSpec((2 * per, ny, nz), lambda i: (i, 0, 0))
    return pl.pallas_call(
        functools.partial(add_kernel, per),
        out_shape=jax.ShapeDtypeStruct((nx, ny, nz), f32),
        grid=(mx // per,),
        in_specs=[block, pl.BlockSpec(q.shape, lambda i: (0, 0, 0, 0))],
        out_specs=block,
        scratch_shapes=[pltpu.VMEM((per + 1, nt, ny, LANES), f32)],
    )(smooth, q)


def solution(mesh):
    placed = (P(*AXES), P(*AXES))
    sizes = tuple(mesh.shape[a] for a in AXES)
    return jax.shard_map(
        functools.partial(on_device, sizes), mesh=mesh, in_specs=placed, out_specs=P(*AXES), check_vma=False
    )
```

profile of v0, /device:TPU:13, one launch (start us, length us, event | category | flops | bytes accessed | tf_op | source)
XLA Modules:
  0.0 100.7 jit_solution(10846402351631838774)
XLA Ops:
  0.0 92.2 %shard_map.28 = (f32[64,64,256]{2,1,0:T(8,128)S(1)}, f32[33,2,40,128]{3,2,1,0:T(8,128)S(1)}) custom-call(f32[64,64,256]{2,1,0:T(8,128)} %start_hbm.1, f32[64,64,256]{2,1,0:T(8,128)} %right_hbm.1), custom_call_target="tpu_custom_call" | custom-call | tf_op jit(solution)/shard_map/pallas_call | solution.py:409
  92.3 0.0 copy-start
  92.3 1.9 %copy-done = f32[64,64,256]{2,1,0:T(8,128)} copy-done((f32[64,64,256]{2,1,0:T(8,128)}, f32[64,64,256]{2,1,0:T(8,128)S(1)}, u32[]{:S(2)}) %copy-start) | copy-done | bytes 4194328
  94.2 0.0 copy-start.1
  94.2 1.1 %copy-done.1 = f32[33,2,40,128]{3,2,1,0:T(8,128)} copy-done((f32[33,2,40,128]{3,2,1,0:T(8,128)}, f32[33,2,40,128]{3,2,1,0:T(8,128)S(1)}, u32[]{:S(2)}) %copy-start.1) | copy-done | bytes 1351704
  95.3 5.4 %shard_map.29 = f32[64,64,256]{2,1,0:T(8,128)} custom-call(f32[64,64,256]{2,1,0:T(8,128)} %copy-done, f32[33,2,40,128]{3,2,1,0:T(8,128)} %copy-done.1), custom_call_target="tpu_custom_call" | custom-call | tf_op jit(solution)/shard_map/pallas_call | solution.py:435
Async XLA Ops:
  92.3 1.9 %copy-start = (f32[64,64,256]{2,1,0:T(8,128)}, f32[64,64,256]{2,1,0:T(8,128)S(1)}, u32[]{:S(2)}) copy-start(f32[64,64,256]{2,1,0:T(8,128)S(1)} %get-tuple-element.7.smooth_ref) | copy-start | bytes 12582916
  94.2 1.1 %copy-start.1 = (f32[33,2,40,128]{3,2,1,0:T(8,128)}, f32[33,2,40,128]{3,2,1,0:T(8,128)S(1)}, u32[]{:S(2)}) copy-start(f32[33,2,40,128]{3,2,1,0:T(8,128)S(1)} %get-tuple-element.8.q_ref) | copy-start | bytes 4055044
where the time goes:
time: 101 us
  Pallas kernels  97.7 us (97%)
  local copies, waits for them, and re-layouts  2.99 us (3%)
    pallas_call x1, Pallas kernels, on_device(): pl.pallas_call(functools.partial(correct_kernel, sizes), out_shape=(jax.S...  92.2 us
    pallas_call x1, Pallas kernels, on_device(): pl.pallas_call(functools.partial(add_kernel, per), out_shape=jax.ShapeDty...  5.42 us
    unnamed x4, local copies, waits for them, and re-layouts  2.99 us

commit v1 on v0

v1 whole, which is shorter than its diff:
```python
import functools

import jax
import jax.numpy as jnp
from jax import lax
from jax.experimental import pallas as pl
from jax.experimental.pallas import tpu as pltpu
from jax.sharding import PartitionSpec as P

FINE_SWEEPS = 2
COARSE_SWEEPS = 4
OMEGA = 6.0 / 7.0
STEP = OMEGA / 1.5
LANES = 128
PAD = 8
AXES = ("gx", "gy", "gz")
MESH = pl.DeviceIdType.MESH

FACES = ((1, 0, 0), (-1, 0, 0), (0, 1, 0), (0, -1, 0), (0, 0, 1), (0, 0, -1))
EDGES = ((0, 1, 1), (1, 1, 0), (1, 0, 1), (1, 1, 1))
NEIGHBOURS = FACES + EDGES + tuple(tuple(-c for c in d) for d in EDGES)
N_COPIES = 10 * (FINE_SWEEPS + 1) + 4 + 6 * (COARSE_SWEEPS - 1) + 7


def rotated(values, shift):
    return pltpu.roll(values, shift, 1)


def split_dot(values, matrix):
    high = values.astype(jnp.bfloat16)
    rest = values - high.astype(jnp.float32)
    middle = rest.astype(jnp.bfloat16)
    low = (rest - middle.astype(jnp.float32)).astype(jnp.bfloat16)
    total = jnp.dot(low, matrix, preferred_element_type=jnp.float32)
    total = total + jnp.dot(middle, matrix, preferred_element_type=jnp.float32)
    return total + jnp.dot(high, matrix, preferred_element_type=jnp.float32)


def correct_kernel(
    sizes, start_hbm, right_hbm, u2, q_ref,
    u0, u1, f, ys, yr, zs, zr, zm, rs, rr, px, py, rys, ryr, rdr, rzs, rzr, rhs,
    c0, c1, c2, c3, cys, cyr, czs, czr, czm, xyr, xzr, yzr, xyzr, ze,
    local_sem, send_sem, recv_sem,
):
    nt, nx, ny, _ = f.shape
    mx, my = nx // 2, ny // 2
    half = nx // 2
    me = tuple(lax.axis_index(a) for a in AXES)

    def lanes(rows):
        return lax.broadcasted_iota(jnp.int32, (rows, LANES), 1)

    lane, lane_c = lanes(ny), lanes(my)

    def there(d):
        found = None
        for at, step, size in zip(me, d, sizes):
            if step:
                one = at < size - 1 if step > 0 else at > 0
                found = one if found is None else jnp.logical_and(found, one)
        return found

    def minus(d):
        return tuple(-c for c in d)

    def device(d):
        return tuple(at + step for at, step in zip(me, d))

    sent = []

    def send(src, dst, d):
        number = len(sent)

        def copy(to):
            return pltpu.make_async_remote_copy(
                src_ref=src, dst_ref=dst, send_sem=send_sem.at[number],
                recv_sem=recv_sem.at[number], device_id=device(to), device_id_type=MESH)

        @pl.when(there(d))
        def _():
            copy(d).start()

        sent.append((copy, d, dst))
        return number

    def arrive(number):
        copy, d, dst = sent[number]

        @pl.when(there(minus(d)))
        def _():
            copy(minus(d)).wait_recv()

        @pl.when(jnp.logical_not(there(minus(d))))
        def _():
            dst[...] = jnp.zeros(dst.shape, dst.dtype)

    loads = []
    for into, source in ((u0, start_hbm), (f, right_hbm)):
        for h in range(2):
            for t in range(nt):
                rows = pl.ds(h * half, half)
                to = f.at[t, rows] if into is f else u0.at[t, pl.ds(1 + h * half, half), pl.ds(PAD, ny), :]
                loads.append(pltpu.make_async_copy(
                    source.at[rows, :, pl.ds(t * LANES, LANES)], to, local_sem.at[len(loads)]))
    for load in loads:
        load.start()

    barrier = pltpu.get_barrier_semaphore()
    expected = jnp.int32(0)
    for d in NEIGHBOURS:
        @pl.when(there(d))
        def _():
            pl.semaphore_signal(barrier, inc=1, device_id=device(d), device_id_type=MESH)
        expected = expected + there(d).astype(jnp.int32)
    zs[...] = jnp.zeros(zs.shape, zs.dtype)
    czs[...] = jnp.zeros(czs.shape, czs.dtype)
    pl.semaphore_wait(barrier, expected)

    mid = pl.ds(PAD, ny)

    def pack_lanes(ref, at, place, first, last):
        rows = first.shape[0]
        index = lanes(rows)
        both = rotated(jnp.where(index == LANES - 1, last, first), 2 * place + 1)
        chosen = jnp.logical_or(index == 2 * place, index == 2 * place + 1)
        ref[at] = jnp.where(chosen, both, ref[at])

    def merge_lanes(low, high):
        index = lanes(low.shape[0])
        return jnp.where(lax.rem(index, 2) == 0, low, rotated(high, LANES - 2))

    def pack_fine(k, h, x, planes):
        for t in range(nt):
            ys[k, 0, t, pl.ds(x, 1), :] = planes[t][0:1, :]
            ys[k, 1, t, pl.ds(x, 1), :] = planes[t][ny - 1:ny, :]
        pack_lanes(zs, (k, h), x - h * half, planes[0], planes[nt - 1])

    def send_low(u):
        return send(u.at[:, 1, mid, :], u.at[:, nx + 1, mid, :], (-1, 0, 0))

    def send_high(u):
        return send(u.at[:, nx, mid, :], u.at[:, 0, mid, :], (1, 0, 0))

    def send_yz(k, h):
        rows = pl.ds(h * half, half)
        return [
            send(ys.at[k, 1, :, rows, :], yr.at[k, 0, :, rows, :], (0, 1, 0)),
            send(ys.at[k, 0, :, rows, :], yr.at[k, 1, :, rows, :], (0, -1, 0)),
            send(zs.at[k, h], zr.at[k, h, 0], (0, 0, 1)),
            send(zs.at[k, h], zr.at[k, h, 1], (0, 0, -1)),
        ]

    def fill_fine(u, k, h, waits):
        for number in waits:
            arrive(number)
        zm[k, h] = merge_lanes(zr[k, h, 0], zr[k, h, 1])

        def rows(x, _):
            for t in range(nt):
                u[t, x + 1, PAD - 1:PAD, :] = yr[k, 0, t, pl.ds(x, 1), :]
                u[t, x + 1, PAD + ny:PAD + ny + 1, :] = yr[k, 1, t, pl.ds(x, 1), :]
            return 0
        lax.fori_loop(h * half, (h + 1) * half, rows, 0, unroll=4)

    def around(u, k, h, x):
        sums = []
        outer = rotated(zm[k, h], lax.rem(LANES - 2 * (x - h * half), LANES))
        planes = [u[t, x + 1, mid, :] for t in range(nt)]
        left = [rotated(p, 1) for p in planes]
        right = [rotated(p, LANES - 1) for p in planes]
        for t in range(nt):
            before = jnp.where(lane == 0, left[t - 1] if t else outer, left[t])
            after = jnp.where(lane == LANES - 1, right[t + 1] if t < nt - 1 else outer, right[t])
            total = u[t, x, mid, :] + u[t, x + 2, mid, :]
            total = total + u[t, x + 1, PAD - 1:PAD - 1 + ny, :] + u[t, x + 1, PAD + 1:PAD + 1 + ny, :]
            sums.append(total + before + after)
        return planes, sums

    waits_yz, low_arrival, high_arrival = [None, None], None, None
    for h in range(2):
        for load in loads[h * nt:(h + 1) * nt]:
            load.wait()

        def pack_start(j, _, h=h):
            for x in (2 * j, 2 * j + 1):
                pack_fine(0, h, x, [u0[t, x + 1, mid, :] for t in range(nt)])
            return 0

        lax.fori_loop(h * half // 2, (h + 1) * half // 2, pack_start, 0)
        waits_yz[h] = send_yz(0, h)
        if h == 0:
            high_arrival = send_low(u0)
        else:
            low_arrival = send_high(u0)
    for load in loads[2 * nt:]:
        load.wait()

    fields = (u0, u1, u2)
    for k in range(FINE_SWEEPS):
        old, new = fields[k], fields[k + 1]

        def pair(j, h, old=old, new=new, k=k):
            for x in (2 * j, 2 * j + 1):
                planes, sums = around(old, k, h, x)
                results = []
                for t in range(nt):
                    value = (planes[t] + f[t, x] + sums[t]) * (1.0 - OMEGA)
                    new[t, x + 1, mid, :] = value
                    results.append(value)
                pack_fine(k + 1, h, x, results)

        next_yz = [None, None]
        fill_fine(old, k, 0, waits_yz[0])
        lax.fori_loop(1, half // 2, lambda j, _: (pair(j, 0), 0)[1], 0)
        arrive(low_arrival)
        pair(0, 0)
        next_yz[0] = send_yz(k + 1, 0)
        next_high = send_low(new)
        arrive(high_arrival)
        fill_fine(old, k, 1, waits_yz[1])
        lax.fori_loop(half // 2, nx // 2, lambda j, _: (pair(j, 1), 0)[1], 0)
        next_yz[1] = send_yz(k + 1, 1)
        low_arrival, high_arrival = send_high(new), next_high
        waits_yz = next_yz

    smooth = fields[FINE_SWEEPS]
    k_last = FINE_SWEEPS

    def residual(x, h):
        planes, sums = around(smooth, k_last, h, x)
        return tuple(f[t, x] - 6.0 * planes[t] + sums[t] for t in range(nt))

    def restrict_x(at, even, odd, following):
        for t in range(nt):
            value = 0.25 * even[t] + 0.5 * odd[t] + 0.25 * following[t]
            px[t, at, 0:ny, :] = value
            rys[t, pl.ds(at, 1), :] = value[0:1, :]

    def step_x(i, following, h):
        even, odd = residual(2 * i, h), residual(2 * i + 1, h)
        restrict_x(i, even, odd, following)
        return even

    middle = half // 2
    fill_fine(smooth, k_last, 0, waits_yz[0])
    following = lax.fori_loop(
        0, middle - 2, lambda j, c: step_x(middle - 2 - j, c, 0), residual(half - 2, 0))
    arrive(low_arrival)
    first = step_x(0, following, 0)
    for t in range(nt):
        rs[t] = first[t]
    rx = send(rs, rr, (-1, 0, 0))
    arrive(high_arrival)
    fill_fine(smooth, k_last, 1, waits_yz[1])
    following = lax.fori_loop(
        0, mx - 1 - middle, lambda j, c: step_x(mx - 2 - j, c, 1), residual(nx - 2, 1))
    step_x(middle - 1, following, 0)
    arrive(rx)
    step_x(mx - 1, [rr[t] for t in range(nt)], 1)
    ry = send(rys, ryr, (0, -1, 0))
    rd = send(rys, rdr, (0, -1, -1))

    def weights(fine, coarse, scale):
        gap = fine - 2 * coarse
        outer = jnp.logical_or(gap == 0, gap == 2)
        value = jnp.where(gap == 1, 0.5 * scale, jnp.where(outer, 0.25 * scale, 0.0))
        return value.astype(jnp.bfloat16)

    nz = nt * LANES
    down = weights(
        lax.broadcasted_iota(jnp.int32, (nz, LANES), 0), lax.broadcasted_iota(jnp.int32, (nz, LANES), 1), 1.0)
    up = weights(
        lax.broadcasted_iota(jnp.int32, (LANES, nz), 1), lax.broadcasted_iota(jnp.int32, (LANES, nz), 0), 2.0)
    last_row = lax.broadcasted_iota(jnp.int32, (my, LANES), 0) == my - 1

    def step_y(i, pack):
        for t in range(nt):
            evens = px[t, i, pl.ds(0, my, stride=2), :]
            odds = px[t, i, pl.ds(1, my, stride=2), :]
            nexts = jnp.where(last_row, 0.0, pltpu.roll(evens, my - 1, 0))
            part = 0.25 * evens + 0.5 * odds + 0.25 * nexts
            py[i, :, t * LANES:(t + 1) * LANES] = part
            if t == 0:
                pack = jnp.where(lane_c == i, rotated(part, i), pack)
        return pack

    zero_c = jnp.zeros((my, LANES), jnp.float32)
    rzs[...] = lax.fori_loop(0, mx, step_y, zero_c, unroll=4)
    rz = send(rzs, rzr, (0, 0, -1))
    group = 4 if mx % 4 == 0 else 1

    def step_z(i, _):
        at = pl.ds(i * group, group)
        block = py[at].reshape(group * my, nz)
        rhs[at] = split_dot(block, down).reshape(group, my, LANES)
        return 0

    lax.fori_loop(0, mx // group, step_z, 0)

    mid_c = pl.ds(PAD, my)

    def pack_coarse(k, i, plane):
        cys[k, 0, pl.ds(i, 1), :] = plane[0:1, :]
        cys[k, 1, pl.ds(i, 1), :] = plane[my - 1:my, :]
        pack_lanes(czs, k, i, plane, plane)

    def send_coarse(c, k):
        return [
            send(c.at[mx, mid_c, :], c.at[0, mid_c, :], (1, 0, 0)),
            send(c.at[1, mid_c, :], c.at[mx + 1, mid_c, :], (-1, 0, 0)),
            send(cys.at[k, 1], cyr.at[k, 0], (0, 1, 0)),
            send(cys.at[k, 0], cyr.at[k, 1], (0, -1, 0)),
            send(czs.at[k], czr.at[k, 0], (0, 0, 1)),
            send(czs.at[k], czr.at[k, 1], (0, 0, -1)),
        ]

    for number in (ry, rd, rz):
        arrive(number)
    beyond = jnp.where(lanes(mx) == LANES - 1, 0.0625 * rotated(rdr[0], LANES - 1), 0.0)
    beyond = beyond + 0.25 * split_dot(jnp.concatenate([ryr[t] for t in range(nt)], 1), down)
    cys[0, 0] = beyond

    def finish_rhs(i, _):
        outside = 0.25 * rotated(rzr[...], LANES - 1 - i)
        value = rhs[i] + jnp.where(lane_c == LANES - 1, outside, 0.0)
        value = value + jnp.where(last_row, cys[0, 0, pl.ds(i, 1), :], 0.0)
        value = value * STEP
        rhs[i] = value
        c0[i + 1, mid_c, :] = value
        pack_coarse(0, i, value)
        return 0

    lax.fori_loop(0, mx, finish_rhs, 0, unroll=4)
    grids = (c0, c1, c2, c3)
    waits = send_coarse(c0, 0)
    for k in range(COARSE_SWEEPS - 1):
        old, new = grids[k], grids[k + 1]
        for number in waits:
            arrive(number)
        czm[k] = merge_lanes(czr[k, 0], czr[k, 1])

        def rows(i, _):
            old[i + 1, PAD - 1:PAD, :] = cyr[k, 0, pl.ds(i, 1), :]
            old[i + 1, PAD + my:PAD + my + 1, :] = cyr[k, 1, pl.ds(i, 1), :]
            return 0

        lax.fori_loop(0, mx, rows, 0, unroll=8)

        def sweep_c(i, _):
            outer = rotated(czm[k], lax.rem(LANES - 2 * i, LANES))
            plane = old[i + 1, mid_c, :]
            total = old[i, mid_c, :] + old[i + 2, mid_c, :]
            total = total + old[i + 1, PAD - 1:PAD - 1 + my, :] + old[i + 1, PAD + 1:PAD + 1 + my, :]
            total = total + jnp.where(lane_c == 0, outer, rotated(plane, 1))
            total = total + jnp.where(lane_c == LANES - 1, outer, rotated(plane, LANES - 1))
            value = (1.0 - 1.5 * STEP) * plane + rhs[i] + (0.25 * STEP) * total
            new[i + 1, mid_c, :] = value
            pack_coarse(k + 1, i, value)
            return 0

        lax.fori_loop(0, mx, sweep_c, 0, unroll=4)
        if k < COARSE_SWEEPS - 2:
            waits = send_coarse(new, k + 1)

    k = COARSE_SWEEPS - 1
    last = grids[k]
    waits = [
        send(last.at[mx, mid_c, :], last.at[0, mid_c, :], (1, 0, 0)),
        send(cys.at[k, 1], cyr.at[k, 0], (0, 1, 0)),
        send(czs.at[k], czr.at[k, 0], (0, 0, 1)),
        send(cys.at[k, 1], xyr, (1, 1, 0)),
        send(czs.at[k], xzr, (1, 0, 1)),
        send(czs.at[k], yzr, (0, 1, 1)),
        send(czs.at[k], xyzr, (1, 1, 1)),
    ]
    for number in waits:
        arrive(number)
    turn = LANES - 2 * (mx - 1)
    inside = jnp.where(lane_c == 0, rotated(xzr[...], turn), rotated(czr[k, 0], 2))
    corner = jnp.where(lane_c == 0, rotated(xyzr[...], turn), rotated(yzr[...], 2))
    ze[mid_c, :] = inside
    ze[0:PAD, :] = corner[my - PAD:my, :]
    below = jnp.zeros((PAD, LANES), jnp.float32)
    last[0, 0:PAD, :] = jnp.broadcast_to(xyr[mx - 1:mx, :], (PAD, LANES))
    last[0, PAD + my:, :] = below

    def rows_last(i, _):
        last[i + 1, 0:PAD, :] = jnp.broadcast_to(cyr[k, 0, pl.ds(i, 1), :], (PAD, LANES))
        last[i + 1, PAD + my:, :] = below
        return 0

    lax.fori_loop(0, mx, rows_last, 0, unroll=8)
    rows_e = my + 2 * PAD
    lane_e = lanes(my + PAD)
    three = 3 if (mx + 1) % 3 == 0 else 1

    def prolong_z(j, _):
        block = last[pl.ds(j * three, three)].reshape(three * rows_e, LANES)
        value = split_dot(block, up)
        for g in range(three):
            outside = 0.5 * rotated(ze[...], lax.rem(LANES - 2 * (j * three + g), LANES))
            for t in range(nt):
                part = value[g * rows_e:g * rows_e + my + PAD, t * LANES:(t + 1) * LANES]
                if t == 0:
                    part = part + jnp.where(lane_e == 0, outside, 0.0)
                q_ref[j * three + g, t] = part
        return 0

    lax.fori_loop(0, (mx + 1) // three, prolong_z, 0)

    for copy, d, _ in sent:
        @pl.when(there(d))
        def _():
            copy(d).wait_send()


def add_kernel(per, smooth_ref, q_ref, out_hbm, both, out_ref, sems):
    mx, nt, my = q_ref.shape[0] - 1, q_ref.shape[1], q_ref.shape[2] - PAD
    ny = 2 * my

    def spread(p, _):
        for t in range(nt):
            here = q_ref[p, t, PAD:PAD + my, :]
            before = q_ref[p, t, PAD - 1:PAD - 1 + my, :]
            both[p, t, pl.ds(0, my, stride=2), :] = 0.5 * (before + here)
            both[p, t, pl.ds(1, my, stride=2), :] = here
        return 0

    def add(j, _):
        for t in range(nt):
            part = pl.ds(t * LANES, LANES)
            here = both[j + 1, t]
            first = smooth_ref[t, 2 * j + 1, PAD:PAD + ny, :]
            second = smooth_ref[t, 2 * j + 2, PAD:PAD + ny, :]
            out_ref[2 * j, :, part] = first + 0.5 * (both[j, t] + here)
            out_ref[2 * j + 1, :, part] = second + here
        return 0

    copies = []
    spread(0, 0)
    for c in range(mx // per):
        lax.fori_loop(c * per + 1, (c + 1) * per + 1, spread, 0, unroll=2)
        lax.fori_loop(c * per, (c + 1) * per, add, 0)
        rows = pl.ds(2 * c * per, 2 * per)
        copies.append(pltpu.make_async_copy(out_ref.at[rows], out_hbm.at[rows], sems.at[c]))
        copies[-1].start()
    for copy in copies:
        copy.wait()


def on_device(sizes, start_field, right_side):
    nx, ny, nz = start_field.shape
    nt, mx, my = nz // LANES, nx // 2, ny // 2
    f32 = jnp.float32
    fine_shape = (nt, nx + 2, ny + 2 * PAD, LANES)
    fine = pltpu.VMEM(fine_shape, f32)
    coarse = pltpu.VMEM((mx + 2, my + 2 * PAD, LANES), f32)
    rounds = FINE_SWEEPS + 1
    y_faces = pltpu.VMEM((rounds, 2, nt, nx, LANES), f32)
    z_pairs = pltpu.VMEM((rounds, 2, ny, LANES), f32)
    x_plane = pltpu.VMEM((nt, ny, LANES), f32)
    y_rows = pltpu.VMEM((nt, mx, LANES), f32)
    z_pack = pltpu.VMEM((my, LANES), f32)
    vmem = pl.BlockSpec(memory_space=pltpu.VMEM)
    smooth, q = pl.pallas_call(
        functools.partial(correct_kernel, sizes),
        out_shape=(
            pltpu.VMEM(fine_shape, f32),
            pltpu.VMEM((mx + 1, nt, my + PAD, LANES), f32),
        ),
        in_specs=[pl.BlockSpec(memory_space=pltpu.HBM)] * 2,
        out_specs=(vmem, vmem),
        scratch_shapes=[
            fine, fine, pltpu.VMEM((nt, nx, ny, LANES), f32),
            y_faces, y_faces, z_pairs, pltpu.VMEM((rounds, 2, 2, ny, LANES), f32), z_pairs,
            x_plane, x_plane, pltpu.VMEM((nt, mx, ny, LANES), f32), pltpu.VMEM((mx, my, nz), f32),
            y_rows, y_rows, y_rows, z_pack, z_pack, pltpu.VMEM((mx, my, LANES), f32),
            coarse, coarse, coarse, coarse,
            pltpu.VMEM((COARSE_SWEEPS, 2, mx, LANES), f32), pltpu.VMEM((COARSE_SWEEPS, 2, mx, LANES), f32),
            pltpu.VMEM((COARSE_SWEEPS, my, LANES), f32), pltpu.VMEM((COARSE_SWEEPS, 2, my, LANES), f32),
            pltpu.VMEM((COARSE_SWEEPS, my, LANES), f32),
            pltpu.VMEM((mx, LANES), f32), z_pack, z_pack, z_pack, pltpu.VMEM((my + PAD, LANES), f32),
            pltpu.SemaphoreType.DMA((4 * nt,)),
            pltpu.SemaphoreType.DMA((N_COPIES,)),
            pltpu.SemaphoreType.DMA((N_COPIES,)),
        ],
        compiler_params=pltpu.CompilerParams(
            collective_id=0, has_side_effects=True, vmem_limit_bytes=40 * 1024 * 1024),
    )(*(pltpu.with_memory_space_constraint(a, pltpu.HBM) for a in (start_field, right_side)))
    per = 8 if mx % 8 == 0 else 1
    return pl.pallas_call(
        functools.partial(add_kernel, per),
        out_shape=jax.ShapeDtypeStruct((nx, ny, nz), f32),
        in_specs=[vmem, vmem],
        out_specs=pl.BlockSpec(memory_space=pl.ANY),
        scratch_shapes=[
            pltpu.VMEM((mx + 1, nt, ny, LANES), f32), pltpu.VMEM((nx, ny, nz), f32),
            pltpu.SemaphoreType.DMA((mx // per,)),
        ],
        compiler_params=pltpu.CompilerParams(vmem_limit_bytes=24 * 1024 * 1024),
    )(smooth, q)


def solution(mesh):
    placed = (P(*AXES), P(*AXES))
    sizes = tuple(mesh.shape[a] for a in AXES)
    return jax.shard_map(
        functools.partial(on_device, sizes), mesh=mesh, in_specs=placed, out_specs=P(*AXES), check_vma=False
    )
```

time: 101 us -> 57 us (0.56)
  Pallas kernels: 97.7 us -> 56.9 us
  local copies, waits for them, and re-layouts: 2.99 us -> 0 us
    pallas_call x1, Pallas kernels: 92.2 us -> 54.6 us  [on_device(): pl.pallas_call(functools.partial(correct_kernel, sizes), out_shape=(pltpu...]
    pallas_call x1, Pallas kernels: 5.42 us -> 2.25 us  [on_device(): pl.pallas_call(functools.partial(add_kernel, per), out_shape=jax.ShapeDty...]
    unnamed x4 -> x0, local copies, waits for them, and re-layouts: 2.99 us -> none
where the time goes in v1:
time: 57 us; the launch traced here: 56.9 us
  Pallas kernels  56.9 us (100%)
    pallas_call x1, Pallas kernels, on_device(): pl.pallas_call(functools.partial(correct_kernel, sizes), out_shape=(pltpu...  54.6 us
    pallas_call x1, Pallas kernels, on_device(): pl.pallas_call(functools.partial(add_kernel, per), out_shape=jax.ShapeDty...  2.25 us

profile of v1, /device:TPU:13, one launch (start us, length us, event | category | flops | bytes accessed | tf_op | source)
XLA Modules:
  0.0 56.9 jit_solution(2513022018037863258)
XLA Ops:
  0.0 54.6 %shard_map.28 = (f32[2,66,80,128]{3,2,1,0:T(8,128)S(1)}, f32[33,2,40,128]{3,2,1,0:T(8,128)S(1)}) custom-call(f32[64,64,256]{2,1,0:T(8,128)} %start_hbm.1, f32[64,64,256]{2,1,0:T(8,128)} %right_hbm.1), custom_call_target="tpu_custom_call" | custom-call | tf_op jit(solution)/shard_map/pallas_call | solution.py:465
  54.6 2.2 %shard_map.29 = f32[64,64,256]{2,1,0:T(8,128)} custom-call(f32[2,66,80,128]{3,2,1,0:T(8,128)S(1)} %get-tuple-element.7.smooth_ref, f32[33,2,40,128]{3,2,1,0:T(8,128)S(1)} %get-tuple-element.8.q_ref), custom_call_target="tpu_custom_call" | custom-call | tf_op jit(solution)/shard_map/pallas_call | solution.py:491

commit v2 on v1

--- a/solution.py
+++ b/solution.py
@@ -13,6 +13,7 @@
 STEP = OMEGA / 1.5
 LANES = 128
 PAD = 8
+ROWS = 16
 AXES = ("gx", "gy", "gz")
 MESH = pl.DeviceIdType.MESH
 
@@ -38,7 +39,7 @@
 
 def correct_kernel(
     sizes, start_hbm, right_hbm, u2, q_ref,
-    u0, u1, f, ys, yr, zs, zr, zm, rs, rr, px, py, rys, ryr, rdr, rzs, rzr, rhs,
+    u0, u1, f, ys, yr, zs, zr, zm, rk, rs, rr, px, py, rys, ryr, rdr, rzs, rzr, rhs,
     c0, c1, c2, c3, cys, cyr, czs, czr, czm, xyr, xzr, yzr, xyzr, ze,
     local_sem, send_sem, recv_sem,
 ):
@@ -119,8 +120,7 @@
     mid = pl.ds(PAD, ny)
 
     def pack_lanes(ref, at, place, first, last):
-        rows = first.shape[0]
-        index = lanes(rows)
+        index = lanes(first.shape[0])
         both = rotated(jnp.where(index == LANES - 1, last, first), 2 * place + 1)
         chosen = jnp.logical_or(index == 2 * place, index == 2 * place + 1)
         ref[at] = jnp.where(chosen, both, ref[at])
@@ -129,11 +129,16 @@
         index = lanes(low.shape[0])
         return jnp.where(lax.rem(index, 2) == 0, low, rotated(high, LANES - 2))
 
-    def pack_fine(k, h, x, planes):
+    block = ROWS if ny % ROWS == 0 else ny
+    blocks = range(0, ny, block)
+
+    def pack_fine(k, h, x, row, planes):
         for t in range(nt):
-            ys[k, 0, t, pl.ds(x, 1), :] = planes[t][0:1, :]
-            ys[k, 1, t, pl.ds(x, 1), :] = planes[t][ny - 1:ny, :]
-        pack_lanes(zs, (k, h), x - h * half, planes[0], planes[nt - 1])
+            if row == 0:
+                ys[k, 0, t, pl.ds(x, 1), :] = planes[t][0:1, :]
+            if row == ny - block:
+                ys[k, 1, t, pl.ds(x, 1), :] = planes[t][block - 1:block, :]
+        pack_lanes(zs, (k, h, pl.ds(row, block)), x - h * half, planes[0], planes[nt - 1])
 
     def send_low(u):
         return send(u.at[:, 1, mid, :], u.at[:, nx + 1, mid, :], (-1, 0, 0))
@@ -162,17 +167,21 @@
             return 0
         lax.fori_loop(h * half, (h + 1) * half, rows, 0, unroll=4)
 
-    def around(u, k, h, x):
+    lane_b = lanes(block)
+
+    def around(u, k, h, x, row):
         sums = []
-        outer = rotated(zm[k, h], lax.rem(LANES - 2 * (x - h * half), LANES))
-        planes = [u[t, x + 1, mid, :] for t in range(nt)]
+        outer = rotated(zm[k, h, pl.ds(row, block), :], lax.rem(LANES - 2 * (x - h * half), LANES))
+        here = pl.ds(PAD + row, block)
+        planes = [u[t, x + 1, here, :] for t in range(nt)]
         left = [rotated(p, 1) for p in planes]
         right = [rotated(p, LANES - 1) for p in planes]
         for t in range(nt):
-            before = jnp.where(lane == 0, left[t - 1] if t else outer, left[t])
-            after = jnp.where(lane == LANES - 1, right[t + 1] if t < nt - 1 else outer, right[t])
-            total = u[t, x, mid, :] + u[t, x + 2, mid, :]
-            total = total + u[t, x + 1, PAD - 1:PAD - 1 + ny, :] + u[t, x + 1, PAD + 1:PAD + 1 + ny, :]
+            before = jnp.where(lane_b == 0, left[t - 1] if t else outer, left[t])
+            after = jnp.where(lane_b == LANES - 1, right[t + 1] if t < nt - 1 else outer, right[t])
+            total = u[t, x, here, :] + u[t, x + 2, here, :]
+            total = total + u[t, x + 1, pl.ds(PAD - 1 + row, block), :]
+            total = total + u[t, x + 1, pl.ds(PAD + 1 + row, block), :]
             sums.append(total + before + after)
         return planes, sums
 
@@ -183,7 +192,8 @@
 
         def pack_start(j, _, h=h):
             for x in (2 * j, 2 * j + 1):
-                pack_fine(0, h, x, [u0[t, x + 1, mid, :] for t in range(nt)])
+                for row in blocks:
+                    pack_fine(0, h, x, row, [u0[t, x + 1, pl.ds(PAD + row, block), :] for t in range(nt)])
             return 0
 
         lax.fori_loop(h * half // 2, (h + 1) * half // 2, pack_start, 0)
@@ -200,14 +210,15 @@
         old, new = fields[k], fields[k + 1]
 
         def pair(j, h, old=old, new=new, k=k):
-            for x in (2 * j, 2 * j + 1):
-                planes, sums = around(old, k, h, x)
-                results = []
-                for t in range(nt):
-                    value = (planes[t] + f[t, x] + sums[t]) * (1.0 - OMEGA)
-                    new[t, x + 1, mid, :] = value
-                    results.append(value)
-                pack_fine(k + 1, h, x, results)
+            for row in blocks:
+                for x in (2 * j, 2 * j + 1):
+                    planes, sums = around(old, k, h, x, row)
+                    results = []
+                    for t in range(nt):
+                        value = (planes[t] + f[t, x, pl.ds(row, block), :] + sums[t]) * (1.0 - OMEGA)
+                        new[t, x + 1, pl.ds(PAD + row, block), :] = value
+                        results.append(value)
+                    pack_fine(k + 1, h, x, row, results)
 
         next_yz = [None, None]
         fill_fine(old, k, 0, waits_yz[0])
@@ -226,37 +237,43 @@
     smooth = fields[FINE_SWEEPS]
     k_last = FINE_SWEEPS
 
-    def residual(x, h):
-        planes, sums = around(smooth, k_last, h, x)
-        return tuple(f[t, x] - 6.0 * planes[t] + sums[t] for t in range(nt))
-
-    def restrict_x(at, even, odd, following):
+    def residual(x, h, row):
+        planes, sums = around(smooth, k_last, h, x, row)
+        return [f[t, x, pl.ds(row, block), :] - 6.0 * planes[t] + sums[t] for t in range(nt)]
+
+    def keep(ref, row, values):
         for t in range(nt):
-            value = 0.25 * even[t] + 0.5 * odd[t] + 0.25 * following[t]
-            px[t, at, 0:ny, :] = value
-            rys[t, pl.ds(at, 1), :] = value[0:1, :]
-
-    def step_x(i, following, h):
-        even, odd = residual(2 * i, h), residual(2 * i + 1, h)
-        restrict_x(i, even, odd, following)
-        return even
+            ref[t, pl.ds(row, block), :] = values[t]
+
+    def step_x(i, h, ref, out):
+        for row in blocks:
+            even, odd = residual(2 * i, h, row), residual(2 * i + 1, h, row)
+            for t in range(nt):
+                following = ref[t, pl.ds(row, block), :]
+                value = 0.25 * even[t] + 0.5 * odd[t] + 0.25 * following
+                px[t, i, pl.ds(row, block), :] = value
+                if row == 0:
+                    rys[t, pl.ds(i, 1), :] = value[0:1, :]
+            keep(out, row, even)
+
+    def start_x(x, h):
+        for row in blocks:
+            keep(rk, row, residual(x, h, row))
 
     middle = half // 2
     fill_fine(smooth, k_last, 0, waits_yz[0])
-    following = lax.fori_loop(
-        0, middle - 2, lambda j, c: step_x(middle - 2 - j, c, 0), residual(half - 2, 0))
+    start_x(half - 2, 0)
+    lax.fori_loop(0, middle - 2, lambda j, _: (step_x(middle - 2 - j, 0, rk, rk), 0)[1], 0, unroll=2)
     arrive(low_arrival)
-    first = step_x(0, following, 0)
-    for t in range(nt):
-        rs[t] = first[t]
+    step_x(0, 0, rk, rs)
     rx = send(rs, rr, (-1, 0, 0))
     arrive(high_arrival)
     fill_fine(smooth, k_last, 1, waits_yz[1])
-    following = lax.fori_loop(
-        0, mx - 1 - middle, lambda j, c: step_x(mx - 2 - j, c, 1), residual(nx - 2, 1))
-    step_x(middle - 1, following, 0)
+    start_x(nx - 2, 1)
+    lax.fori_loop(0, mx - 1 - middle, lambda j, _: (step_x(mx - 2 - j, 1, rk, rk), 0)[1], 0, unroll=3)
+    step_x(middle - 1, 0, rk, rk)
     arrive(rx)
-    step_x(mx - 1, [rr[t] for t in range(nt)], 1)
+    step_x(mx - 1, 1, rr, rk)
     ry = send(rys, ryr, (0, -1, 0))
     rd = send(rys, rdr, (0, -1, -1))
 
@@ -291,8 +308,7 @@
 
     def step_z(i, _):
         at = pl.ds(i * group, group)
-        block = py[at].reshape(group * my, nz)
-        rhs[at] = split_dot(block, down).reshape(group, my, LANES)
+        rhs[at] = split_dot(py[at].reshape(group * my, nz), down).reshape(group, my, LANES)
         return 0
 
     lax.fori_loop(0, mx // group, step_z, 0)
@@ -358,7 +374,7 @@
             pack_coarse(k + 1, i, value)
             return 0
 
-        lax.fori_loop(0, mx, sweep_c, 0, unroll=4)
+        lax.fori_loop(0, mx, sweep_c, 0, unroll=8)
         if k < COARSE_SWEEPS - 2:
             waits = send_coarse(new, k + 1)
 
@@ -395,8 +411,7 @@
     three = 3 if (mx + 1) % 3 == 0 else 1
 
     def prolong_z(j, _):
-        block = last[pl.ds(j * three, three)].reshape(three * rows_e, LANES)
-        value = split_dot(block, up)
+        value = split_dot(last[pl.ds(j * three, three)].reshape(three * rows_e, LANES), up)
         for g in range(three):
             outside = 0.5 * rotated(ze[...], lax.rem(LANES - 2 * (j * three + g), LANES))
             for t in range(nt):
@@ -473,7 +488,7 @@
         scratch_shapes=[
             fine, fine, pltpu.VMEM((nt, nx, ny, LANES), f32),
             y_faces, y_faces, z_pairs, pltpu.VMEM((rounds, 2, 2, ny, LANES), f32), z_pairs,
-            x_plane, x_plane, pltpu.VMEM((nt, mx, ny, LANES), f32), pltpu.VMEM((mx, my, nz), f32),
+            x_plane, x_plane, x_plane, pltpu.VMEM((nt, mx, ny, LANES), f32), pltpu.VMEM((mx, my, nz), f32),
             y_rows, y_rows, y_rows, z_pack, z_pack, pltpu.VMEM((mx, my, LANES), f32),
             coarse, coarse, coarse, coarse,
             pltpu.VMEM((COARSE_SWEEPS, 2, mx, LANES), f32), pltpu.VMEM((COARSE_SWEEPS, 2, mx, LANES), f32),

time: 57 us -> 54.4 us (0.954)
  Pallas kernels: 56.9 us -> 54.2 us
    pallas_call x1, Pallas kernels: 54.6 us -> 52 us  [on_device(): pl.pallas_call(functools.partial(correct_kernel, sizes), out_shape=(pltpu...]
where the time goes in v2:
time: 54.4 us; the launch traced here: 54.2 us
  Pallas kernels  54.2 us (100%)
    pallas_call x1, Pallas kernels, on_device(): pl.pallas_call(functools.partial(correct_kernel, sizes), out_shape=(pltpu...  52 us
    pallas_call x1, Pallas kernels, on_device(): pl.pallas_call(functools.partial(add_kernel, per), out_shape=jax.ShapeDty...  2.25 us

profile of v2, /device:TPU:13, one launch (start us, length us, event | category | flops | bytes accessed | tf_op | source)
XLA Modules:
  0.0 54.2 jit_solution(15085443828647874931)
XLA Ops:
  0.0 52.0 %shard_map.28 = (f32[2,66,80,128]{3,2,1,0:T(8,128)S(1)}, f32[33,2,40,128]{3,2,1,0:T(8,128)S(1)}) custom-call(f32[64,64,256]{2,1,0:T(8,128)} %start_hbm.1, f32[64,64,256]{2,1,0:T(8,128)} %right_hbm.1), custom_call_target="tpu_custom_call" | custom-call | tf_op jit(solution)/shard_map/pallas_call | solution.py:480
  52.0 2.2 %shard_map.29 = f32[64,64,256]{2,1,0:T(8,128)} custom-call(f32[2,66,80,128]{3,2,1,0:T(8,128)S(1)} %get-tuple-element.7.smooth_ref, f32[33,2,40,128]{3,2,1,0:T(8,128)S(1)} %get-tuple-element.8.q_ref), custom_call_target="tpu_custom_call" | custom-call | tf_op jit(solution)/shard_map/pallas_call | solution.py:506
